TPU v7x, 32 devices: a whole 2x2x4 slice. The times are simulated.
32 devices in a mesh: pts: 8 (over z, y), cent: 4 (over x, core).
Axes of the slice: x: 2, y: 2, z: 4, core: 2. Of those that a mesh axis runs over, the one named last changes fastest.
Arguments:
- points: bfloat16 [65536, 512], P(('pts', 'cent')), may hold values from -128 to 128
- centroids: bfloat16 [8192, 512], P('pts'), may hold values from -32 to 32
- candidates: int32 [4096, 2], P(('pts', 'cent')), may hold values from 0 to 31, all different within a row; in each aligned block of 128 rows (0 to 127, 128 to 255, ...) at most 9 rows name the same one
Outputs:
- new_centroids: bfloat16 [8192, 512], P('pts')
- point_lse: float32 [65536], P(('pts', 'cent'))
Inputs may be any that keep to these rules, and one draw needn't show every extreme that they name: `candidates`: within the 128 point blocks of one device, no centroid block is named more than 9 times; the two ids of a point block differ.
All inputs are finite; a program needn't handle non-finite values.
Results may differ from a plain program's by a relative error of at most 0.006.
Values may be sent and summed in bfloat16 or wider, within the bound.
A program may use at most 64 MiB of HBM per device.

v0:
```python
import functools
import math

import jax
import jax.numpy as jnp
from jax import lax
from jax.experimental import pallas as pl
from jax.experimental.pallas import tpu as pltpu
from jax.sharding import PartitionSpec as P

CB = 256
PB = 16
ITERS = 2


def stable_lse(scores, reduce_axis):
    highest = jnp.max(scores, axis=reduce_axis, keepdims=True)
    summed = jnp.sum(jnp.exp(scores - highest), axis=reduce_axis)
    return jnp.squeeze(highest, reduce_axis) + jnp.log(summed)


def pick_kernel(home_block, grouped, outgoing):
    @pl.loop(0, outgoing.shape[0])
    def _(slot):
        outgoing[slot] = grouped[home_block[slot]]


def pick_blocks(home_block, grouped):
    vmem = pl.BlockSpec(memory_space=pltpu.VMEM)
    return pl.pallas_call(
        pick_kernel,
        out_shape=jax.ShapeDtypeStruct(home_block.shape + grouped.shape[1:], grouped.dtype),
        in_specs=[pl.BlockSpec(memory_space=pltpu.SMEM), vmem],
        out_specs=vmem,
        compiler_params=pltpu.CompilerParams(vmem_limit_bytes=32 << 20),
    )(home_block, grouped)


def swap_kernel(parts, x, out, landed, send_sem, recv_sem):
    me = lax.axis_index("pts")
    barrier = pltpu.get_barrier_semaphore()
    for step in range(1, parts):
        pl.semaphore_signal(
            barrier, inc=1, device_id={"pts": lax.rem(me + step, parts)},
            device_id_type=pl.DeviceIdType.MESH,
        )
    pl.semaphore_wait(barrier, parts - 1)
    copies = []
    for step in range(1, parts):
        peer = lax.rem(me + step, parts)
        copy = pltpu.make_async_remote_copy(
            src_ref=x.at[peer],
            dst_ref=landed.at[me],
            send_sem=send_sem.at[step],
            recv_sem=recv_sem.at[step],
            device_id={"pts": peer},
            device_id_type=pl.DeviceIdType.MESH,
        )
        copy.start()
        copies.append(copy)
    out[me] = x[me]
    for step in range(1, parts):
        copies[step - 1].wait()
        origin = lax.rem(me - step + parts, parts)
        out[origin] = landed[origin]


def swap(values, number):
    held, owners, capacity, width = values.shape
    size = held * capacity * width
    full = -(-size // 1024) * 1024
    flat = jnp.swapaxes(values, 0, 1).reshape(owners, size)
    flat = jnp.pad(flat, ((0, 0), (0, full - size))).reshape(owners, full // 128, 128)
    vmem = pl.BlockSpec(memory_space=pltpu.VMEM)
    result = pl.pallas_call(
        functools.partial(swap_kernel, owners),
        out_shape=jax.ShapeDtypeStruct(flat.shape, flat.dtype),
        in_specs=[vmem],
        out_specs=vmem,
        scratch_shapes=[
            pltpu.VMEM(flat.shape, flat.dtype),
            pltpu.SemaphoreType.DMA((owners,)),
            pltpu.SemaphoreType.DMA((owners,)),
        ],
        compiler_params=pltpu.CompilerParams(collective_id=number, has_side_effects=True),
    )(flat)
    result = result.reshape(owners, full)[:, :size]
    return jnp.swapaxes(result.reshape(owners, held, capacity, width), 0, 1)


def make_scoring(centre_table, centre_norms, inverse_root):

    def scoring(package):
        slot_rows = package
        leading = slot_rows.shape[0]
        flat_rows = slot_rows.reshape(leading, -1, slot_rows.shape[-1])
        products = jnp.einsum(
            "lsd,lmd->lsm", flat_rows, centre_table, preferred_element_type=jnp.float32
        )
        scores = inverse_root * (2.0 * products - centre_norms[:, None, :])
        scores = scores.reshape(slot_rows.shape[:-1] + (centre_table.shape[1],))
        return (scores, stable_lse(scores, scores.ndim - 1))

    return scoring


def on_device(points, centroids, candidates):
    feature_width = points.shape[1]
    inverse_root = 1.0 / math.sqrt(feature_width)
    owners = lax.axis_size("pts")
    held_blocks = centroids.shape[0] // CB
    point_blocks = candidates.shape[0]
    total_blocks = held_blocks * owners
    capacity = max(2, 2 * point_blocks // total_blocks + 1)
    slot_count = held_blocks * owners * capacity
    grouped = points.reshape(point_blocks, PB, feature_width)
    picked = candidates.reshape(-1)
    entry_count = picked.shape[0]
    labels = jnp.arange(total_blocks, dtype=jnp.int32)
    member = (picked[:, None] == labels[None, :]).astype(jnp.bfloat16)
    entry_index = jnp.arange(entry_count, dtype=jnp.int32)
    earlier = (entry_index[None, :] < entry_index[:, None]).astype(jnp.bfloat16)
    prior_hits = jnp.dot(earlier, member, preferred_element_type=jnp.float32)
    arrival = jnp.sum(prior_hits * member.astype(jnp.float32), axis=1).astype(jnp.int32)
    local_block = picked % held_blocks
    target = picked // held_blocks
    position = (local_block * owners + target) * capacity + arrival
    slot_shape = (held_blocks, owners, capacity)
    current = centroids
    places = jnp.arange(slot_count, dtype=jnp.int32)
    source = (
        jnp.sum(
            jnp.where(position[:, None] == places[None, :], entry_index[:, None] + 1, 0), axis=0
        )
        - 1
    )
    filled = source >= 0
    home_block = jnp.maximum(source, 0) // 2
    outgoing = pick_blocks(home_block, grouped)
    outgoing = outgoing.reshape(slot_shape + (PB, feature_width))
    point_lse = jnp.zeros((point_blocks, PB), jnp.float32)
    arrived = lax.all_to_all(outgoing, "pts", split_axis=1, concat_axis=1, tiled=True)
    for iteration in range(ITERS):
        centre_table = current.reshape(-1, CB, feature_width)
        centre_norms = jnp.sum(jnp.square(centre_table.astype(jnp.float32)), axis=2)
        scoring = make_scoring(centre_table, centre_norms, inverse_root)
        scores, partial_value = scoring(arrived)
        returned = swap(partial_value, 2 * iteration)
        per_entry = returned.reshape(slot_count, PB)[position]
        paired = per_entry.reshape(point_blocks, 2, PB)
        point_lse = stable_lse(paired, 1)
        outward = jnp.where(filled[:, None], point_lse[home_block], jnp.float32(1e30))
        outward = outward.reshape(slot_shape + (PB,))
        inward = swap(outward, 2 * iteration + 1)
        weights = jnp.exp(scores - inward[..., None])
        leading = weights.shape[0]
        flat_weights = weights.reshape(leading, -1, CB)
        masses = jnp.sum(flat_weights, axis=1).reshape(leading * CB)
        rounded = flat_weights.astype(jnp.bfloat16)
        flat_rows = arrived.reshape(leading, -1, feature_width)
        weighted = jnp.einsum(
            "lsm,lsd->lmd", rounded, flat_rows, preferred_element_type=jnp.float32
        )
        weighted = weighted.astype(jnp.bfloat16).reshape(leading * CB, feature_width)
        share_sums, share_mass = (
            lax.psum_scatter(weighted, "cent", scatter_dimension=0, tiled=True),
            lax.psum_scatter(masses, "cent", scatter_dimension=0, tiled=True),
        )
        share_rows = share_sums.shape[0]
        first_row = lax.axis_index("cent") * share_rows
        previous = lax.dynamic_slice_in_dim(current, first_row, share_rows, 0).astype(jnp.float32)
        renewed = ((share_sums.astype(jnp.float32) + previous) / (share_mass[:, None] + 1.0)).astype(jnp.bfloat16)
        current = lax.all_gather(renewed, "cent", axis=0, tiled=True)
    return (current, point_lse.reshape(-1))


def solution(mesh):
    return jax.shard_map(
        on_device,
        mesh=mesh,
        in_specs=(P(("pts", "cent"), None), P("pts", None), P(("pts", "cent"), None)),
        out_specs=(P("pts", None), P(("pts", "cent"))),
        check_vma=False,
    )
```

profile of v0, /device:TPU:0, one launch (start us, length us, event | category | flops | bytes accessed | tf_op | source)
XLA Modules:
  0.0 296.5 jit_solution(13038729645586399382)
XLA Ops:
  7.2 0.8 copy.43
  8.5 1.6 copy-done
  10.1 2.2 shard_map.50
  12.3 2.7 copy.44
  15.0 7.4 %all-to-all-start = ((bf16[4,8,9,16,512]{4,3,2,0,1:T(8,128)(2,1)}), bf16[4,8,9,16,512]{4,3,2,0,1:T(8,128)(2,1)}, u32[]{:S(2)}, u32[]{:S(2)}) async-start(bf16[4,8,9,16,512]{4,3,2,0,1:T(8,128)(2,1)} %copy.44), calls=%async_computation | async-start | bytes 9437184 | tf_op jit(solution)/shard_map/all_to_all | solution.py:142
  23.1 103.8 %all-to-all-done = bf16[4,8,9,16,512]{4,3,2,0,1:T(8,128)(2,1)} async-done(((bf16[4,8,9,16,512]{4,3,2,0,1:T(8,128)(2,1)}), bf16[4,8,9,16,512]{4,3,2,0,1:T(8,128)(2,1)}, u32[]{:S(2)}, u32[]{:S(2)}) %all-to-all-start) | async-done | bytes 4718624 | tf_op jit(solution)/shard_map/all_to_all | solution.py:142
  127.0 2.8 copy.45
  129.8 1.7 fusion.30
  131.9 2.2 copy-done.2
  135.7 7.8 %shard_map.51 = f32[8,8,128]{2,1,0:T(8,128)} custom-call(f32[8,8,128]{2,1,0:T(8,128)} %bitcast.92), custom_call_target="tpu_custom_call" | custom-call | tf_op jit(solution)/shard_map/pallas_call | solution.py:75
  143.5 0.8 copy.87
  145.6 1.1 gather_fusion.1
  148.2 7.9 %shard_map.52 = f32[8,8,128]{2,1,0:T(8,128)} custom-call(f32[8,8,128]{2,1,0:T(8,128)} %bitcast.94), custom_call_target="tpu_custom_call" | custom-call | tf_op jit(solution)/shard_map/pallas_call | solution.py:75
  157.1 6.3 %fusion.14 = bf16[4,256,512]{2,1,0:T(8,128)(2,1)} fusion(bf16[4,1152,512]{2,1,0:T(8,128)(2,1)} %bitcast.75, f32[4,1152,256]{1,2,0:T(8,128)} %copy-done.2, f32[4,1152]{1,0:T(4,128)S(1)} %sub.108), kind=kOutput, calls=%fused_computation.24 | convolution fusion | flops 1210843136 | bytes 10504192 | tf_op jit(solution)/shard_map/lsm,lsd->lmd/dot_general | solution.py:161
  164.7 3.0 %fusion.4 = f32[4,256]{1,0:T(4,128)S(1)} fusion(f32[4,1152,256]{1,2,0:T(8,128)} %copy-done.2, f32[4,1152]{1,0:T(4,128)S(1)} %sub.108), kind=kLoop, calls=%fused_computation.14 | loop fusion | flops 2358272 | bytes 4741120 | tf_op jit(solution)/shard_map/reduce_sum | solution.py:158
  167.7 5.7 %all-reduce.4 = f32[1024]{0:T(1024)S(1)} all-reduce(f32[1024]{0:T(1024)S(1)} %bitcast.106), channel_id=3, replica_groups=mesh['pts'=8,'cent'=4] {'cent'}, use_global_device_ids=true, to_apply=%region_9.10.clone | all-reduce | flops 1024 | bytes 8192
  173.5 14.2 %reduce-scatter.3.cloned.1.call-done = bf16[256,512]{1,0:T(8,128)(2,1)} async-done(((bf16[1024,512]{1,0:T(8,128)(2,1)}), bf16[256,512]{1,0:T(8,128)(2,1)}) %reduce-scatter.3.cloned.1.call-update) | async-done | bytes 262160 | tf_op jit(solution)/shard_map/reduce_scatter | solution.py:166
  187.7 1.8 divide_convert_fusion.1
  189.7 16.9 %all-gather.3.cloned.1.call-done = bf16[1024,512]{1,0:T(8,128)(2,1)} async-done(((bf16[256,512]{1,0:T(8,128)(2,1)}), bf16[1024,512]{1,0:T(8,128)(2,1)}) %all-gather.3.cloned.1.call-update) | async-done | bytes 1048592 | tf_op jit(solution)/shard_map/all_gather | solution.py:173
  206.6 1.5 multiply_reduce_fusion
  208.1 4.2 %fusion.31 = (f32[4,1152]{1,0:T(4,128)S(1)}, f32[4,1152,256]{1,2,0:T(8,128)S(1)}) fusion(f32[4,256]{1,0:T(4,128)S(1)} %sub.111, bf16[4,1152,512]{2,1,0:T(8,128)(2,1)} %bitcast.76, bf16[4,256,512]{2,1,0:T(8,128)(2,1)} %bitcast.81), kind=kOutput, calls=%fused_computation.87 | convolution fusion | flops 1212673536 | bytes 10508288 | tf_op jit(solution)/shard_map/lsd,lmd->lsm/dot_general | solution.py:97
  212.3 2.2 copy-done.3
  216.1 8.1 %shard_map.53 = f32[8,8,128]{2,1,0:T(8,128)} custom-call(f32[8,8,128]{2,1,0:T(8,128)} %bitcast.96), custom_call_target="tpu_custom_call" | custom-call | tf_op jit(solution)/shard_map/pallas_call | solution.py:75
  226.2 1.1 gather_fusion.3
  228.8 8.0 %shard_map.54 = f32[8,8,128]{2,1,0:T(8,128)} custom-call(f32[8,8,128]{2,1,0:T(8,128)} %bitcast.98), custom_call_target="tpu_custom_call" | custom-call | tf_op jit(solution)/shard_map/pallas_call | solution.py:75
  237.8 6.3 %fusion.17 = bf16[4,256,512]{2,1,0:T(8,128)(2,1)} fusion(bf16[4,1152,512]{2,1,0:T(8,128)(2,1)} %bitcast.77, f32[4,1152,256]{1,2,0:T(8,128)} %copy-done.3, f32[4,1152]{1,0:T(4,128)S(1)} %sub.118), kind=kOutput, calls=%fused_computation.25 | convolution fusion | flops 1210843136 | bytes 10504192 | tf_op jit(solution)/shard_map/lsm,lsd->lmd/dot_general | solution.py:161
  244.2 3.0 %fusion.6 = f32[4,256]{1,0:T(4,128)S(1)} fusion(f32[4,1152,256]{1,2,0:T(8,128)} %copy-done.3, f32[4,1152]{1,0:T(4,128)S(1)} %sub.118), kind=kLoop, calls=%fused_computation.16 | loop fusion | flops 2358272 | bytes 4741120 | tf_op jit(solution)/shard_map/reduce_sum | solution.py:158
  247.2 6.0 %all-reduce.5 = f32[1024]{0:T(1024)S(1)} all-reduce(f32[1024]{0:T(1024)S(1)} %bitcast.107), channel_id=5, replica_groups=mesh['pts'=8,'cent'=4] {'cent'}, use_global_device_ids=true, to_apply=%region_17.18.clone | all-reduce | flops 1024 | bytes 8192
  253.3 15.8 %reduce-scatter.5.cloned.1.call-done = bf16[256,512]{1,0:T(8,128)(2,1)} async-done(((bf16[1024,512]{1,0:T(8,128)(2,1)}), bf16[256,512]{1,0:T(8,128)(2,1)}) %reduce-scatter.5.cloned.1.call-update) | async-done | bytes 262160 | tf_op jit(solution)/shard_map/reduce_scatter | solution.py:166
  269.0 1.8 divide_convert_fusion
  271.6 16.2 %all-gather.5.cloned.1.call-done = bf16[1024,512]{1,0:T(8,128)(2,1)} async-done(((bf16[256,512]{1,0:T(8,128)(2,1)}), bf16[1024,512]{1,0:T(8,128)(2,1)}) %all-gather.5.cloned.1.call-update) | async-done | bytes 1048592 | tf_op jit(solution)/shard_map/all_gather | solution.py:173
  287.7 2.3 copy.90
  (94 shorter events, 14.8 us)
Async XLA Ops:
  8.5 1.6 copy-start
  15.0 7.6 %copy-start.4 = (bf16[1024,512]{1,0:T(8,128)(2,1)S(1)}, bf16[1024,512]{1,0:T(8,128)(2,1)}, u32[]{:S(2)}) copy-start(bf16[1024,512]{1,0:T(8,128)(2,1)} %param.4) | copy-start | bytes 3145732
  15.0 112.0 %all-to-all-start = ((bf16[4,8,9,16,512]{4,3,2,0,1:T(8,128)(2,1)}), bf16[4,8,9,16,512]{4,3,2,0,1:T(8,128)(2,1)}, u32[]{:S(2)}, u32[]{:S(2)}) async-start(bf16[4,8,9,16,512]{4,3,2,0,1:T(8,128)(2,1)} %copy.44), calls=%async_computation | async-start | bytes 9437184 | tf_op jit(solution)/shard_map/all_to_all | solution.py:142
  22.4 165.2 %reduce-scatter.3.cloned.1.call-start = ((), (), s32[]{:S(2)}) async-start(), calls=%async_computation.3 | async-start | bytes 1310720 | tf_op jit(solution)/shard_map/reduce_scatter | solution.py:166
  129.8 2.1 copy-start.1
  131.9 2.2 copy-start.2
  157.1 6.4 %copy-start.5 = (u32[32]{0:T(128)S(1)}, u32[32]{0:T(128)}, u32[]{:S(2)}) copy-start(u32[32]{0:T(128)} %constant.88) | copy-start | bytes 388
  163.4 43.2 %all-gather.3.cloned.1.call-start = ((), (), s32[]{:S(2)}) async-start(), calls=%async_computation.4 | async-start | bytes 1310720 | tf_op jit(solution)/shard_map/all_gather | solution.py:173
  189.5 79.5 %reduce-scatter.5.cloned.1.call-start = ((), (), s32[]{:S(2)}) async-start(), calls=%async_computation.5 | async-start | bytes 1310720 | tf_op jit(solution)/shard_map/reduce_scatter | solution.py:166
  212.3 2.2 copy-start.3
  244.1 43.6 %all-gather.5.cloned.1.call-start = ((), (), s32[]{:S(2)}) async-start(), calls=%async_computation.6 | async-start | bytes 1310720 | tf_op jit(solution)/shard_map/all_gather | solution.py:173
Sparse Core Ops, SparseCore 0:
  163.5 24.1 reduce-scatter.2
  189.8 16.6 all-gather.2
  244.3 24.7 reduce-scatter.4
  271.0 16.6 all-gather.4
where the time goes:
time: 298 us; the launch traced here: 297 us
  waiting for transfers between devices  167 us (56%)
  Pallas kernels  34 us (11%)
  local copies, waits for them, and re-layouts  28.7 us (10%)
  matrix products  18.7 us (6%)
  between operations  14.8 us (5%)
  other arithmetic  14.1 us (5%)
  blocking collectives  11.6 us (4%)
  starting transfers between devices  7.78 us (3%)
    all_to_all x1, waiting for transfers between devices, on_device(): lax.all_to_all(outgoing, 'pts', split_axis=1, concat_axis=1, tiled=True)  104 us
    all_gather x2, waiting for transfers between devices, on_device(): current = lax.all_gather(renewed, 'cent', axis=0, tiled=True)  33 us
    pallas_call x4, Pallas kernels, swap(): pl.pallas_call(functools.partial(swap_kernel, owners), out_shape=jax.Shap...  31.8 us
    reduce_scatter x2, waiting for transfers between devices, on_device(): lax.psum_scatter(weighted, 'cent', scatter_dimension=0, tiled=True)  30 us
    unnamed x29, local copies, waits for them, and re-layouts  15.6 us
    dot_general x2, matrix products, on_device(): jnp.einsum('lsm,lsd->lmd', rounded, flat_rows, preferred_element_type=jnp...  12.6 us
    unnamed x2, blocking collectives  11.6 us
    all_to_all x1, starting transfers between devices, on_device(): lax.all_to_all(outgoing, 'pts', split_axis=1, concat_axis=1, tiled=True)  7.44 us
  transfers between devices with their start and end apart: 5, of which 5 were waited for; matrix products, arithmetic and copies ran while one was open for 3% of the time, Pallas kernels for 0%

commit v1 on v0

v1 whole, which is shorter than its diff:
```python
import functools
import math

import jax
import jax.numpy as jnp
from jax import lax
from jax.experimental import pallas as pl
from jax.experimental.pallas import tpu as pltpu
from jax.sharding import PartitionSpec as P

CB = 256
PB = 16
ITERS = 2
LANES = 128
GROUP = LANES // PB
CHUNKS = 4
MESH = pl.DeviceIdType.MESH
FAR = 1e30


class Plan:
    def __init__(self, pts, cent, point_blocks, width):
        self.pts, self.cent, self.blocks, self.width = pts, cent, point_blocks, width
        self.half = pts // 2
        self.spots = self.half * cent
        self.total = 2 * self.spots
        self.cap = max(2, 2 * point_blocks // self.total + 1)
        self.main = self.cap // GROUP * GROUP
        self.rem = self.cap - self.main
        self.main_rows = self.main // GROUP
        self.rows = self.main_rows + (self.rem > 0)
        self.share = GROUP // self.rem if self.rem else 1
        self.slots = self.total * self.cap
        self.held = self.spots * self.cap
        self.groups = self.held // GROUP
        self.tiles = self.groups // 2
        self.tile_blocks = 2 * GROUP
        assert GROUP % max(self.rem, 1) == 0 and 2 * self.rows <= 8
        assert self.spots & (self.spots - 1) == 0 and self.held % self.tile_blocks == 0

    def pair_order(self):
        pairs = self.spots // 2
        if pairs == 8:
            return (7, 3, 4, 5, 2, 1, 6, 0)
        return tuple(reversed(range(pairs)))


def flip(value, mask):
    out, bit = 0, 1
    while bit <= mask or bit == 1:
        here = (value // bit) % 2
        out = out + bit * ((1 - here) if mask & bit else here)
        bit *= 2
    return out + (value // bit) * bit


def split3(x):
    hi = x.astype(jnp.bfloat16)
    left = x - hi.astype(jnp.float32)
    mid = left.astype(jnp.bfloat16)
    low = (left - mid.astype(jnp.float32)).astype(jnp.bfloat16)
    return jnp.concatenate([hi, mid, low], axis=1)


def pick_rows(onehot, packed):
    out = jnp.dot(onehot, packed, preferred_element_type=jnp.float32)
    return (out[:, :LANES] + out[:, LANES : 2 * LANES]) + out[:, 2 * LANES :]


def iota(shape, axis):
    return lax.broadcasted_iota(jnp.int32, shape, axis)


def to_column(row, start, size):
    parts = []
    for first in range(0, size, LANES):
        part = min(LANES, size - first)
        piece = row[:, start + first : start + first + LANES]
        same = iota((part, LANES), 0) == iota((part, LANES), 1)
        parts.append(jnp.sum(jnp.where(same, piece, 0.0), axis=1, keepdims=True))
    return jnp.concatenate(parts, axis=0)


def to_row(column):
    parts = []
    for first in range(0, column.shape[0], LANES):
        same = iota((LANES, LANES), 0) == iota((LANES, LANES), 1)
        parts.append(jnp.sum(jnp.where(same, column[first : first + LANES], 0.0), axis=0, keepdims=True))
    return jnp.concatenate(parts, axis=1)


def kernel(
    pn, inverse_root, home, table, points, cent_in, new_out, lse_out,
    stage, recv, cents, norms, escr, mrow, lrow, acc, macc,
    pick, pick_lane, back, fill,
    pmsg, pin, lmsg, lin, xout, xin, mout, min_, xout2, xin2, mout2, min2,
    main_s, main_r, rem_s, rem_r, cent_sem, cs, cr, ps, pr, ls, lr,
    xs, xr, ms, mr, x2s, x2r, m2s, m2r, fs, fr,
):
    p, c = lax.axis_index("pts"), lax.axis_index("cent")
    side = p // pn.half
    other = 1 - side
    q = (p % pn.half) * pn.cent + c
    Q = pn.spots

    def device(spot):
        return {"pts": side * pn.half + spot // pn.cent, "cent": spot % pn.cent}

    partner = {"pts": other * pn.half + p % pn.half, "cent": c}

    def remote(src, dst, send, recv_sem, to):
        return pltpu.make_async_remote_copy(
            src_ref=src, dst_ref=dst, send_sem=send, recv_sem=recv_sem,
            device_id=to, device_id_type=MESH,
        )

    barrier = pltpu.get_barrier_semaphore()
    for mask in range(1, Q):
        pl.semaphore_signal(barrier, inc=1, device_id=device(flip(q, mask)), device_id_type=MESH)
    pl.semaphore_signal(barrier, inc=1, device_id=partner, device_id_type=MESH)
    own_copy = pltpu.make_async_copy(cent_in.at[c], cents.at[side], cent_sem)
    own_copy.start()

    masks = [2 * pair + low for pair in pn.pair_order() for low in (0, 1)]

    def gather(mask):
        spot = flip(q, mask)
        for sel in range(2):
            first = (sel * Q + spot) * pn.cap

            @pl.loop(0, pn.cap)
            def _(t):
                stage[mask, sel, t] = points[home[first + t]]

    def gather_own():
        for sel in range(2):
            first = (sel * Q + q) * pn.cap
            if pn.main:
                @pl.loop(0, pn.main)
                def _(t):
                    recv[sel, q * pn.main + t] = points[home[first + t]]
            if pn.rem:
                @pl.loop(0, pn.rem)
                def _(t):
                    recv[sel, Q * pn.main + q * pn.rem + t] = points[home[first + pn.main + t]]

    def main_copy(mask, sel, spot_at):
        return remote(
            stage.at[mask, sel, pl.ds(0, pn.main)],
            recv.at[sel, pl.ds(spot_at * pn.main, pn.main)],
            main_s.at[mask, sel], main_r.at[spot_at, sel], device(flip(q, mask)),
        )

    def rem_copy(mask, sel, spot_at):
        return remote(
            stage.at[mask, sel, pl.ds(pn.main, pn.rem)],
            recv.at[sel, pl.ds(Q * pn.main + spot_at * pn.rem, pn.rem)],
            rem_s.at[mask, sel], rem_r.at[spot_at, sel], device(flip(q, mask)),
        )

    def send(mask):
        for sel in range(2):
            if pn.main:
                main_copy(mask, sel, q).start()
            if pn.rem:
                rem_copy(mask, sel, q).start()

    waiting = None
    for mask in masks:
        if mask:
            gather(mask)
            if waiting is None:
                pl.semaphore_wait(barrier, Q)
            else:
                send(waiting)
            waiting = mask
    own_copy.wait()
    send(waiting)
    cent_copy = remote(cents.at[side], cents.at[side], cs, cr, partner)
    cent_copy.start()
    cent_wait = remote(cents.at[other], cents.at[other], cs, cr, partner)
    gather_own()

    lanes = table[...].astype(jnp.float32)
    entries = 2 * pn.blocks
    entry_row = to_column(lanes[0:1], 0, entries)
    entry_lane = to_column(lanes[1:2], 0, entries)
    slot_home = to_column(lanes[2:3], 0, pn.slots)
    pick[...] = (entry_row == iota((entries, 8 * Q), 1).astype(jnp.float32)).astype(jnp.bfloat16)
    lane_group = (iota((entries, LANES), 1) // PB).astype(jnp.float32)
    pick_lane[...] = (entry_lane == lane_group).astype(jnp.float32)
    back[...] = (slot_home == iota((pn.slots, pn.blocks), 1).astype(jnp.float32)).astype(jnp.bfloat16)
    fill[...] = jnp.broadcast_to(jnp.where(slot_home < 0.0, FAR, 0.0), fill.shape)
    pmsg[...] = jnp.zeros_like(pmsg)
    lmsg[...] = jnp.zeros_like(lmsg)

    def set_norm(sel):
        wide = cents[sel].astype(jnp.float32)
        norms[sel] = jnp.broadcast_to(jnp.sum(wide * wide, axis=1, keepdims=True), (CB, LANES))

    def tile_rows(sel, tile):
        block = recv[sel, pl.ds(tile * pn.tile_blocks, pn.tile_blocks)]
        return block.reshape(pn.tile_blocks * PB, pn.width)

    def score_tile(sel, tile):
        products = lax.dot_general(
            cents[sel], tile_rows(sel, tile), (((1,), (1,)), ((), ())),
            preferred_element_type=jnp.float32,
        )
        out = []
        for h in range(2):
            scores = inverse_root * (2.0 * products[:, h * LANES : (h + 1) * LANES] - norms[sel])
            highest = jnp.max(scores, axis=0, keepdims=True)
            raised = jnp.exp(scores - highest)
            escr[sel, 2 * tile + h] = raised
            mrow[pl.ds(sel * pn.groups + 2 * tile + h, 1)] = highest
            out.append(highest + jnp.log(jnp.sum(raised, axis=0, keepdims=True)))
        return out

    def score_main(it, sel, tile):
        for h, part in enumerate(score_tile(sel, tile)):
            group = 2 * tile + h
            row = (group // pn.main_rows) * 8 + sel * pn.rows + group % pn.main_rows
            pmsg[it, pl.ds(row, 1)] = part

    main_tiles = Q * pn.main_rows // 2

    def score_rem(it, sel, tile):
        for h, part in enumerate(score_tile(sel, tile)):
            first = (2 * tile + h - Q * pn.main_rows) * pn.share
            for s in range(pn.share):
                row = (first + s) * 8 + sel * pn.rows + pn.main_rows
                pmsg[it, pl.ds(row, 1)] = part

    def score_all_rem(it, sel):
        @pl.loop(main_tiles, pn.tiles)
        def _(tile):
            score_rem(it, sel, tile)

    def trade(out, into, send_sem, recv_sem, it):
        into[it, pl.ds(q * 8, 8)] = out[it, pl.ds(q * 8, 8)]
        for mask in masks:
            if mask:
                spot = flip(q, mask)
                remote(
                    out.at[it, pl.ds(spot * 8, 8)], into.at[it, pl.ds(q * 8, 8)],
                    send_sem.at[it, mask], recv_sem.at[it, q], device(spot),
                ).start()
        for mask in masks:
            if mask:
                spot = flip(q, mask)
                copy = remote(
                    out.at[it, pl.ds(spot * 8, 8)], into.at[it, pl.ds(spot * 8, 8)],
                    send_sem.at[it, mask], recv_sem.at[it, spot], device(spot),
                )
                copy.wait()

    def combine(it):
        chosen = pick_rows(pick[...], split3(pin[it]))
        chosen = jnp.where(pick_lane[...] > 0.5, chosen, 0.0)
        step = LANES // 2
        while step >= PB:
            chosen = chosen + pltpu.roll(chosen, step, 1)
            step //= 2
        first, second = chosen[: pn.blocks], chosen[pn.blocks :]
        highest = jnp.maximum(first, second)
        lse = highest + jnp.log(jnp.exp(first - highest) + jnp.exp(second - highest))
        if it == ITERS - 1:
            grouped = lse.reshape(pn.blocks // GROUP, GROUP, LANES)
            shape = grouped.shape
            mine = iota(shape, 2) // PB == iota(shape, 1)
            lse_out[...] = jnp.sum(jnp.where(mine, grouped, 0.0), axis=1)
        spread = pick_rows(back[...], split3(lse)) + fill[...]
        lane = iota((2 * Q, LANES), 1) // PB
        for r in range(pn.rows):
            total = jnp.zeros((2 * Q, LANES), jnp.float32)
            for t in range(pn.cap):
                if (t // GROUP if t < pn.main else pn.main_rows) == r:
                    group = t % GROUP if t < pn.main else (q % pn.share) * pn.rem + t - pn.main
                    total = total + jnp.where(lane == group, spread[t * 2 * Q : (t + 1) * 2 * Q], 0.0)
            for sel in range(2):
                lmsg[it, pl.ds(sel * pn.rows + r, Q, stride=8)] = total[sel * Q : (sel + 1) * Q]

    def unpack(it):
        for sel in range(2):
            base = sel * pn.groups
            for r in range(pn.main_rows):
                rows = lin[it, pl.ds(sel * pn.rows + r, Q, stride=8)]
                if pn.main_rows == 1:
                    lrow[pl.ds(base, Q)] = rows
                else:
                    lrow[pl.ds(base + r, Q, stride=pn.main_rows)] = rows
            if pn.rem:
                rows = lin[it, pl.ds(sel * pn.rows + pn.main_rows, Q, stride=8)]
                joined = jnp.sum(rows.reshape(Q // pn.share, pn.share, LANES), axis=1)
                lrow[pl.ds(base + Q * pn.main_rows, Q // pn.share)] = joined

    def sum_up(sel):
        acc[...] = jnp.zeros_like(acc)
        macc[...] = jnp.zeros_like(macc)

        @pl.loop(0, pn.tiles)
        def _(tile):
            parts = []
            for h in range(2):
                row = sel * pn.groups + 2 * tile + h
                scale = jnp.exp(mrow[pl.ds(row, 1)] - lrow[pl.ds(row, 1)])
                weights = escr[sel, 2 * tile + h] * scale
                macc[...] += weights
                parts.append(weights.astype(jnp.bfloat16))
            acc[...] += jnp.dot(
                jnp.concatenate(parts, axis=1), tile_rows(sel, tile),
                preferred_element_type=jnp.float32,
            )

        return jnp.sum(macc[...], axis=1, keepdims=True)

    set_norm(side)
    cent_wait.wait_recv()
    set_norm(other)

    def wait_main(mask):
        spot = flip(q, mask)
        for sel in range(2):
            main_copy(mask, sel, spot).wait_recv()

    for pair in pn.pair_order()[-1:] + pn.pair_order()[:-1]:
        if pn.main:
            for low in (0, 1):
                if 2 * pair + low:
                    wait_main(2 * pair + low)
            if pn.main_rows == 1:
                tile = flip(q, 2 * pair) // 2

                @pl.loop(0, 2)
                def _(sel):
                    score_main(0, sel, tile)
    if pn.main_rows > 1:
        for sel in range(2):
            @pl.loop(0, main_tiles)
            def _(tile):
                score_main(0, sel, tile)
    if pn.rem:
        for mask in masks:
            if mask:
                for sel in range(2):
                    rem_copy(mask, sel, flip(q, mask)).wait_recv()
        for sel in range(2):
            score_all_rem(0, sel)
    trade(pmsg, pin, ps, pr, 0)
    combine(0)
    trade(lmsg, lin, ls, lr, 0)
    unpack(0)

    def x_copy(sel):
        return remote(xout.at[sel], xin.at[sel], xs.at[sel], xr.at[sel], partner)

    def m_copy(sel):
        return remote(mout.at[sel], min_.at[sel], ms.at[sel], mr.at[sel], partner)

    for sel in (other, side):
        mass = sum_up(sel)
        mout[sel] = jnp.broadcast_to(to_row(mass), (8, CB))
        xout[sel] = acc[...].astype(jnp.bfloat16)
        m_copy(sel).start()
        x_copy(sel).start()

    def renewed(sums, mass, old):
        return ((sums + old.astype(jnp.float32)) / (mass + 1.0)).astype(jnp.bfloat16)

    cent_copy.wait_send()
    for sel in (side, other):
        m_copy(sel).wait_recv()
        x_copy(sel).wait_recv()
        mass = to_column(mout[sel][0:1] + min_[sel][0:1], 0, CB)
        both = xout[sel].astype(jnp.float32) + xin[sel].astype(jnp.float32)
        cents[sel] = renewed(both, mass, cents[sel])
        set_norm(sel)
        if pn.main:
            @pl.loop(0, main_tiles)
            def _(tile):
                score_main(1, sel, tile)
        if pn.rem:
            score_all_rem(1, sel)

    trade(pmsg, pin, ps, pr, 1)
    combine(1)
    trade(lmsg, lin, ls, lr, 1)
    unpack(1)
    rows = CB // CHUNKS

    def x2_copy(k):
        part = pl.ds(k * rows, rows)
        return remote(xout2.at[part], xin2.at[part], x2s.at[k], x2r.at[k], partner)

    m2_copy = remote(mout2, min2, m2s, m2r, partner)
    mass = sum_up(other)
    mout2[...] = jnp.broadcast_to(to_row(mass), (8, CB))
    xout2[...] = acc[...].astype(jnp.bfloat16)
    m2_copy.start()
    for k in range(CHUNKS):
        x2_copy(k).start()
    mass = sum_up(side)
    m2_copy.wait_recv()
    mass = mass + to_column(min2[0:1], 0, CB)

    def f_copy(step, k, spot):
        part = new_out.at[spot, pl.ds(k * rows, rows)]
        to = {"pts": p, "cent": (c + step) % pn.cent}
        return remote(part, part, fs.at[step, k], fr.at[spot, k], to)

    for k in range(CHUNKS):
        part = pl.ds(k * rows, rows)
        x2_copy(k).wait_recv()
        sums = acc[part] + xin2[part].astype(jnp.float32)
        new_out[c, part] = renewed(sums, mass[k * rows : (k + 1) * rows], cents[side, part])
        for step in range(1, pn.cent):
            f_copy(step, k, c).start()

    for mask in masks:
        if mask:
            for sel in range(2):
                if pn.main:
                    main_copy(mask, sel, q).wait_send()
                if pn.rem:
                    rem_copy(mask, sel, q).wait_send()
    for sel in range(2):
        m_copy(sel).wait_send()
        x_copy(sel).wait_send()
    m2_copy.wait_send()
    for k in range(CHUNKS):
        x2_copy(k).wait_send()
        for step in range(1, pn.cent):
            f_copy(step, k, c).wait_send()
            f_copy(step, k, (c - step + pn.cent) % pn.cent).wait_recv()


def tables(pn, candidates):
    q = (lax.axis_index("pts") % pn.half) * pn.cent + lax.axis_index("cent")
    picked = candidates.T.reshape(-1)
    count = picked.shape[0]
    index = jnp.arange(count, dtype=jnp.int32)
    labels = jnp.arange(pn.total, dtype=jnp.int32)
    member = (picked[:, None] == labels[None, :]).astype(jnp.bfloat16)
    earlier = (index[None, :] < index[:, None]).astype(jnp.bfloat16)
    prior = jnp.dot(earlier, member, preferred_element_type=jnp.float32)
    turn = jnp.sum(prior * member.astype(jnp.float32), axis=1).astype(jnp.int32)
    place = picked * pn.cap + turn
    spot, sel = picked % pn.spots, picked // pn.spots
    in_main = turn < pn.main
    row = spot * 8 + sel * pn.rows + jnp.where(in_main, turn // GROUP, pn.main_rows)
    lane = jnp.where(in_main, turn % GROUP, (q % pn.share) * pn.rem + turn - pn.main)
    places = jnp.arange(pn.slots, dtype=jnp.int32)
    block = index % pn.blocks
    source = jnp.sum(jnp.where(place[:, None] == places[None, :], block[:, None] + 1, 0), axis=0) - 1
    by_turn = source.reshape(pn.total, pn.cap).T.reshape(-1)
    width = -(-max(count, pn.slots) // LANES) * LANES

    def row_of(values):
        return jnp.pad(values, (0, width - values.shape[0]))[None]

    rows = jnp.concatenate([row_of(row), row_of(lane), row_of(by_turn)], axis=0)
    table = jnp.pad(rows, ((0, 5), (0, 0)))
    return jnp.maximum(source, 0), table


def on_device(points, centroids, candidates):
    width = points.shape[1]
    pn = Plan(lax.axis_size("pts"), lax.axis_size("cent"), candidates.shape[0], width)
    assert centroids.shape[0] == pn.cent * CB
    home, table = tables(pn, candidates)
    Q, bf16, f32 = pn.spots, jnp.bfloat16, jnp.float32
    vmem = pl.BlockSpec(memory_space=pltpu.VMEM)
    dma = pltpu.SemaphoreType.DMA
    new, lse = pl.pallas_call(
        functools.partial(kernel, pn, 1.0 / math.sqrt(width)),
        out_shape=(
            jax.ShapeDtypeStruct((pn.cent, CB, width), bf16),
            jax.ShapeDtypeStruct((pn.blocks // GROUP, LANES), f32),
        ),
        in_specs=[pl.BlockSpec(memory_space=pltpu.SMEM), vmem, vmem, pl.BlockSpec(memory_space=pl.ANY)],
        out_specs=(vmem, vmem),
        scratch_shapes=[
            pltpu.VMEM((Q, 2, pn.cap, PB, width), bf16),
            pltpu.VMEM((2, pn.held, PB, width), bf16),
            pltpu.VMEM((2, CB, width), bf16),
            pltpu.VMEM((2, CB, LANES), f32),
            pltpu.VMEM((2, pn.groups, CB, LANES), f32),
            pltpu.VMEM((2 * pn.groups, LANES), f32),
            pltpu.VMEM((2 * pn.groups, LANES), f32),
            pltpu.VMEM((CB, width), f32),
            pltpu.VMEM((CB, LANES), f32),
            pltpu.VMEM((2 * pn.blocks, 8 * Q), bf16),
            pltpu.VMEM((2 * pn.blocks, LANES), f32),
            pltpu.VMEM((pn.slots, pn.blocks), bf16),
            pltpu.VMEM((pn.slots, LANES), f32),
            pltpu.VMEM((ITERS, 8 * Q, LANES), f32),
            pltpu.VMEM((ITERS, 8 * Q, LANES), f32),
            pltpu.VMEM((ITERS, 8 * Q, LANES), f32),
            pltpu.VMEM((ITERS, 8 * Q, LANES), f32),
            pltpu.VMEM((2, CB, width), bf16),
            pltpu.VMEM((2, CB, width), bf16),
            pltpu.VMEM((2, 8, CB), f32),
            pltpu.VMEM((2, 8, CB), f32),
            pltpu.VMEM((CB, width), bf16),
            pltpu.VMEM((CB, width), bf16),
            pltpu.VMEM((8, CB), f32),
            pltpu.VMEM((8, CB), f32),
            dma((Q, 2)), dma((Q, 2)), dma((Q, 2)), dma((Q, 2)),
            dma, dma, dma,
            dma((ITERS, Q)), dma((ITERS, Q)), dma((ITERS, Q)), dma((ITERS, Q)),
            dma((2,)), dma((2,)), dma((2,)), dma((2,)),
            dma((CHUNKS,)), dma((CHUNKS,)), dma, dma,
            dma((pn.cent, CHUNKS)), dma((pn.cent, CHUNKS)),
        ],
        compiler_params=pltpu.CompilerParams(
            collective_id=0, has_side_effects=True, vmem_limit_bytes=60 << 20
        ),
    )(home, table, points.reshape(pn.blocks, PB, width), centroids.reshape(pn.cent, CB, width))
    return new.reshape(centroids.shape), lse.reshape(-1)


def solution(mesh):
    return jax.shard_map(
        on_device,
        mesh=mesh,
        in_specs=(P(("pts", "cent"), None), P("pts", None), P(("pts", "cent"), None)),
        out_specs=(P("pts", None), P(("pts", "cent"))),
        check_vma=False,
    )
```

time: 298 us -> 154 us (0.52)
  waiting for transfers between devices: 167 us -> 0 us
  Pallas kernels: 34 us -> 147 us
  local copies, waits for them, and re-layouts: 28.7 us -> 3.76 us
  matrix products: 18.7 us -> 0.96 us
  between operations: 14.8 us -> 0.73 us
  other arithmetic: 14.1 us -> 1.44 us
  blocking collectives: 11.6 us -> 0 us
  starting transfers between devices: 7.78 us -> 0 us
    pallas_call x5 -> x1, Pallas kernels: 34 us -> 147 us  [on_device(): pl.pallas_call(functools.partial(kernel, pn, 1.0 / math.sqrt(width)), out...]
    all_to_all x1 -> x0, waiting for transfers between devices: 104 us -> none  [on_device(): lax.all_to_all(outgoing, 'pts', split_axis=1, concat_axis=1, tiled=True)]
    all_gather x2 -> x0, waiting for transfers between devices: 33 us -> none  [on_device(): current = lax.all_gather(renewed, 'cent', axis=0, tiled=True)]
    reduce_scatter x2 -> x0, waiting for transfers between devices: 30 us -> none  [on_device(): lax.psum_scatter(weighted, 'cent', scatter_dimension=0, tiled=True)]
    dot_general x5 -> x1, matrix products: 18.7 us -> 0.96 us  [tables(): prior = jnp.dot(earlier, member, preferred_element_type=jnp.float32)]
    unnamed x29 -> x4, local copies, waits for them, and re-layouts: 15.6 us -> 2.87 us
    unnamed x2 -> x0, blocking collectives: 11.6 us -> none
    reduce_sum x9 -> x1, other arithmetic: 9.75 us -> 0.15 us  [tables(): jnp.sum(jnp.where(place[:, None] == places[None, :], block[:, None] + 1,...]
  transfers between devices with their start and end apart: 5 -> 0, of which waited for: 5 -> 0; matrix products, arithmetic and copies ran while one was open for 3% -> 0% of each run, Pallas kernels for 0% -> 0%
where the time goes in v1:
time: 154 us
  Pallas kernels  147 us (95%)
  local copies, waits for them, and re-layouts  3.76 us (2%)
    pallas_call x1, Pallas kernels, on_device(): pl.pallas_call(functools.partial(kernel, pn, 1.0 / math.sqrt(width)), out...  147 us

profile of v1, /device:TPU:0, one launch (start us, length us, event | category | flops | bytes accessed | tf_op | source)
XLA Modules:
  0.0 153.5 jit_solution(11576745494048951110)
XLA Ops:
  0.7 1.0 fusion
  1.6 0.7 fusion.6
  2.3 0.1 select_reduce_fusion
  2.5 0.6 broadcast_add_fusion
  3.1 0.1 sub.23
  3.2 0.1 copy.6
  3.3 0.1 reshape.48
  3.4 0.6 pad.18.table
  4.0 146.6 %shard_map.50 = (bf16[4,256,512]{2,1,0:T(8,128)(2,1)}, f32[16,128]{1,0:T(8,128)}) custom-call(s32[288]{0:T(512)} %get-tuple-element.9.home, s32[8,384]{1,0:T(8,128)} %pad.18.table, bf16[128,16,512]{2,1,0:T(8,128)(2,1)} %bitcast.10, bf16[4,256,512]{2,1,0:T(8,128)(2,1)} %bitcast.11), custom_call_target="tpu_custom_call" | custom-call | tf_op jit(solution)/shard_map/pallas_call | solution.py:475
  150.6 0.0 copy-start
  150.6 2.3 %copy.9 = bf16[1024,512]{1,0:T(8,128)(2,1)} copy(bf16[1024,512]{1,0:T(8,128)(2,1)} %bitcast.12) | data formatting | bytes 2097152
  152.9 0.0 copy-done
  152.9 0.6 copy.10
  (7 shorter events, 0.0 us)
Async XLA Ops:
  150.6 2.3 %copy-start = (f32[16,128]{1,0:T(8,128)S(1)}, f32[16,128]{1,0:T(8,128)}, u32[]{:S(2)}) copy-start(f32[16,128]{1,0:T(8,128)} %get-tuple-element.5) | copy-start | bytes 24580

commit v2 on v1

--- a/solution.py
+++ b/solution.py
@@ -13,7 +13,10 @@
 ITERS = 2
 LANES = 128
 GROUP = LANES // PB
-CHUNKS = 4
+CHUNKS = 8
+SPARE = 12 << 20
+LOG2E = math.log2(math.e)
+LN2 = math.log(2.0)
 MESH = pl.DeviceIdType.MESH
 FAR = 1e30
 
@@ -91,7 +94,7 @@
 
 def kernel(
     pn, inverse_root, home, table, points, cent_in, new_out, lse_out,
-    stage, recv, cents, norms, escr, mrow, lrow, acc, macc,
+    stage, recv, cents, norms, escr, wscr, mrow, lrow, acc, macc,
     pick, pick_lane, back, fill,
     pmsg, pin, lmsg, lin, xout, xin, mout, min_, xout2, xin2, mout2, min2,
     main_s, main_r, rem_s, rem_r, cent_sem, cs, cr, ps, pr, ls, lr,
@@ -128,7 +131,7 @@
         for sel in range(2):
             first = (sel * Q + spot) * pn.cap
 
-            @pl.loop(0, pn.cap)
+            @pl.loop(0, pn.cap, unroll=pn.cap)
             def _(t):
                 stage[mask, sel, t] = points[home[first + t]]
 
@@ -196,7 +199,8 @@
 
     def set_norm(sel):
         wide = cents[sel].astype(jnp.float32)
-        norms[sel] = jnp.broadcast_to(jnp.sum(wide * wide, axis=1, keepdims=True), (CB, LANES))
+        total = jnp.sum(wide * wide, axis=1, keepdims=True)
+        norms[sel] = jnp.broadcast_to((inverse_root * LOG2E) * total, (CB, LANES))
 
     def tile_rows(sel, tile):
         block = recv[sel, pl.ds(tile * pn.tile_blocks, pn.tile_blocks)]
@@ -209,12 +213,12 @@
         )
         out = []
         for h in range(2):
-            scores = inverse_root * (2.0 * products[:, h * LANES : (h + 1) * LANES] - norms[sel])
+            scores = (2.0 * inverse_root * LOG2E) * products[:, h * LANES : (h + 1) * LANES] - norms[sel]
             highest = jnp.max(scores, axis=0, keepdims=True)
-            raised = jnp.exp(scores - highest)
+            raised = jnp.exp2(scores - highest)
             escr[sel, 2 * tile + h] = raised
             mrow[pl.ds(sel * pn.groups + 2 * tile + h, 1)] = highest
-            out.append(highest + jnp.log(jnp.sum(raised, axis=0, keepdims=True)))
+            out.append(LN2 * highest + jnp.log(jnp.sum(raised, axis=0, keepdims=True)))
         return out
 
     def score_main(it, sel, tile):
@@ -296,23 +300,21 @@
                 lrow[pl.ds(base + Q * pn.main_rows, Q // pn.share)] = joined
 
     def sum_up(sel):
-        acc[...] = jnp.zeros_like(acc)
         macc[...] = jnp.zeros_like(macc)
-
-        @pl.loop(0, pn.tiles)
+        rows = pn.tile_blocks * PB
+
+        @pl.loop(0, pn.tiles, unroll=3)
         def _(tile):
-            parts = []
             for h in range(2):
                 row = sel * pn.groups + 2 * tile + h
-                scale = jnp.exp(mrow[pl.ds(row, 1)] - lrow[pl.ds(row, 1)])
+                scale = jnp.exp2(mrow[pl.ds(row, 1)] - LOG2E * lrow[pl.ds(row, 1)])
                 weights = escr[sel, 2 * tile + h] * scale
                 macc[...] += weights
-                parts.append(weights.astype(jnp.bfloat16))
-            acc[...] += jnp.dot(
-                jnp.concatenate(parts, axis=1), tile_rows(sel, tile),
-                preferred_element_type=jnp.float32,
-            )
-
+                wscr[:, pl.ds(pl.multiple_of(tile * rows + h * LANES, LANES), LANES)] = weights.astype(jnp.bfloat16)
+
+        acc[...] = jnp.dot(
+            wscr[...], recv[sel].reshape(pn.held * PB, pn.width), preferred_element_type=jnp.float32
+        )
         return jnp.sum(macc[...], axis=1, keepdims=True)
 
     set_norm(side)
@@ -332,8 +334,7 @@
             if pn.main_rows == 1:
                 tile = flip(q, 2 * pair) // 2
 
-                @pl.loop(0, 2)
-                def _(sel):
+                for sel in range(2):
                     score_main(0, sel, tile)
     if pn.main_rows > 1:
         for sel in range(2):
@@ -377,7 +378,7 @@
         cents[sel] = renewed(both, mass, cents[sel])
         set_norm(sel)
         if pn.main:
-            @pl.loop(0, main_tiles)
+            @pl.loop(0, main_tiles, unroll=2)
             def _(tile):
                 score_main(1, sel, tile)
         if pn.rem:
@@ -472,6 +473,35 @@
     Q, bf16, f32 = pn.spots, jnp.bfloat16, jnp.float32
     vmem = pl.BlockSpec(memory_space=pltpu.VMEM)
     dma = pltpu.SemaphoreType.DMA
+    buffers = [
+        ((Q, 2, pn.cap, PB, width), bf16),
+        ((2, pn.held, PB, width), bf16),
+        ((2, CB, width), bf16),
+        ((2, CB, LANES), f32),
+        ((2, pn.groups, CB, LANES), f32),
+        ((CB, pn.held * PB), bf16),
+        ((2 * pn.groups, LANES), f32),
+        ((2 * pn.groups, LANES), f32),
+        ((CB, width), f32),
+        ((CB, LANES), f32),
+        ((2 * pn.blocks, 8 * Q), bf16),
+        ((2 * pn.blocks, LANES), f32),
+        ((pn.slots, pn.blocks), bf16),
+        ((pn.slots, LANES), f32),
+        ((ITERS, 8 * Q, LANES), f32),
+        ((ITERS, 8 * Q, LANES), f32),
+        ((ITERS, 8 * Q, LANES), f32),
+        ((ITERS, 8 * Q, LANES), f32),
+        ((2, CB, width), bf16),
+        ((2, CB, width), bf16),
+        ((2, 8, CB), f32),
+        ((2, 8, CB), f32),
+        ((CB, width), bf16),
+        ((CB, width), bf16),
+        ((8, CB), f32),
+        ((8, CB), f32),
+    ]
+    taken = sum(math.prod(shape) * jnp.dtype(kind).itemsize for shape, kind in buffers)
     new, lse = pl.pallas_call(
         functools.partial(kernel, pn, 1.0 / math.sqrt(width)),
         out_shape=(
@@ -480,32 +510,7 @@
         ),
         in_specs=[pl.BlockSpec(memory_space=pltpu.SMEM), vmem, vmem, pl.BlockSpec(memory_space=pl.ANY)],
         out_specs=(vmem, vmem),
-        scratch_shapes=[
-            pltpu.VMEM((Q, 2, pn.cap, PB, width), bf16),
-            pltpu.VMEM((2, pn.held, PB, width), bf16),
-            pltpu.VMEM((2, CB, width), bf16),
-            pltpu.VMEM((2, CB, LANES), f32),
-            pltpu.VMEM((2, pn.groups, CB, LANES), f32),
-            pltpu.VMEM((2 * pn.groups, LANES), f32),
-            pltpu.VMEM((2 * pn.groups, LANES), f32),
-            pltpu.VMEM((CB, width), f32),
-            pltpu.VMEM((CB, LANES), f32),
-            pltpu.VMEM((2 * pn.blocks, 8 * Q), bf16),
-            pltpu.VMEM((2 * pn.blocks, LANES), f32),
-            pltpu.VMEM((pn.slots, pn.blocks), bf16),
-            pltpu.VMEM((pn.slots, LANES), f32),
-            pltpu.VMEM((ITERS, 8 * Q, LANES), f32),
-            pltpu.VMEM((ITERS, 8 * Q, LANES), f32),
-            pltpu.VMEM((ITERS, 8 * Q, LANES), f32),
-            pltpu.VMEM((ITERS, 8 * Q, LANES), f32),
-            pltpu.VMEM((2, CB, width), bf16),
-            pltpu.VMEM((2, CB, width), bf16),
-            pltpu.VMEM((2, 8, CB), f32),
-            pltpu.VMEM((2, 8, CB), f32),
-            pltpu.VMEM((CB, width), bf16),
-            pltpu.VMEM((CB, width), bf16),
-            pltpu.VMEM((8, CB), f32),
-            pltpu.VMEM((8, CB), f32),
+        scratch_shapes=[pltpu.VMEM(*buffer) for buffer in buffers] + [
             dma((Q, 2)), dma((Q, 2)), dma((Q, 2)), dma((Q, 2)),
             dma, dma, dma,
             dma((ITERS, Q)), dma((ITERS, Q)), dma((ITERS, Q)), dma((ITERS, Q)),
@@ -514,7 +519,7 @@
             dma((pn.cent, CHUNKS)), dma((pn.cent, CHUNKS)),
         ],
         compiler_params=pltpu.CompilerParams(
-            collective_id=0, has_side_effects=True, vmem_limit_bytes=60 << 20
+            collective_id=0, has_side_effects=True, vmem_limit_bytes=taken + SPARE
         ),
     )(home, table, points.reshape(pn.blocks, PB, width), centroids.reshape(pn.cent, CB, width))
     return new.reshape(centroids.shape), lse.reshape(-1)

time: 154 us -> 147 us (0.955)
  Pallas kernels: 147 us -> 139 us
    pallas_call x1, Pallas kernels: 147 us -> 139 us  [on_device(): pl.pallas_call(functools.partial(kernel, pn, 1.0 / math.sqrt(width)), out...]
    unnamed x4 -> x6, local copies, waits for them, and re-layouts: 2.87 us -> 4.38 us
where the time goes in v2:
time: 147 us
  Pallas kernels  139 us (95%)
  local copies, waits for them, and re-layouts  4.67 us (3%)
    pallas_call x1, Pallas kernels, on_device(): pl.pallas_call(functools.partial(kernel, pn, 1.0 / math.sqrt(width)), out...  139 us
    unnamed x6, local copies, waits for them, and re-layouts  4.38 us

profile of v2, /device:TPU:0, one launch (start us, length us, event | category | flops | bytes accessed | tf_op | source)
XLA Modules:
  0.0 146.6 jit_solution(17846527633425835117)
XLA Ops:
  0.7 1.0 fusion
  1.6 0.7 fusion.6
  2.3 0.1 select_reduce_fusion
  2.5 0.1 sub.23
  2.6 0.1 copy.6
  2.7 0.1 reshape.48
  2.8 0.0 copy-start
  2.8 1.6 %copy-done = bf16[2048,512]{1,0:T(8,128)(2,1)S(1)} copy-done((bf16[2048,512]{1,0:T(8,128)(2,1)S(1)}, bf16[2048,512]{1,0:T(8,128)(2,1)}, u32[]{:S(2)}) %copy-start) | copy-done | bytes 2097176
  4.4 0.0 copy-start.1
  4.4 1.2 copy-done.1
  5.7 139.3 %shard_map.50 = (bf16[4,256,512]{2,1,0:T(8,128)(2,1)S(1)}, f32[16,128]{1,0:T(8,128)S(1)}) custom-call(s32[288]{0:T(512)S(1)} %get-tuple-element.9.home, s32[8,384]{1,0:T(8,128)S(1)} %pad.18.table, bf16[128,16,512]{2,1,0:T(8,128)(2,1)S(1)} %bitcast.10, bf16[4,256,512]{2,1,0:T(8,128)(2,1)S(1)} %bitcast.11), custom_call_target="tpu_custom_call" | custom-call | tf_op jit(solution)/shard_map/pallas_call | solution.py:505
  145.0 1.0 copy.9
  146.0 0.6 copy.10
  (9 shorter events, 0.1 us)
Async XLA Ops:
  2.8 1.6 %copy-start = (bf16[2048,512]{1,0:T(8,128)(2,1)S(1)}, bf16[2048,512]{1,0:T(8,128)(2,1)}, u32[]{:S(2)}) copy-start(bf16[2048,512]{1,0:T(8,128)(2,1)} %param.3) | copy-start | bytes 6291460
  4.4 1.2 copy-start.1

commit v3 on v2

--- a/solution.py
+++ b/solution.py
@@ -93,11 +93,11 @@
 
 
 def kernel(
-    pn, inverse_root, home, table, points, cent_in, new_out, lse_out,
-    stage, recv, cents, norms, escr, wscr, mrow, lrow, acc, macc,
+    pn, inverse_root, named_in, points_in, cent_in, new_out, lse_out,
+    named, points, home_v, home, stage, recv, cents, norms, escr, wscr, mrow, lrow, acc, macc,
     pick, pick_lane, back, fill,
     pmsg, pin, lmsg, lin, xout, xin, mout, min_, xout2, xin2, mout2, min2,
-    main_s, main_r, rem_s, rem_r, cent_sem, cs, cr, ps, pr, ls, lr,
+    named_sem, pts_sem, home_sem, main_s, main_r, rem_s, rem_r, cent_sem, cs, cr, ps, pr, ls, lr,
     xs, xr, ms, mr, x2s, x2r, m2s, m2r, fs, fr,
 ):
     p, c = lax.axis_index("pts"), lax.axis_index("cent")
@@ -117,35 +117,60 @@
             device_id=to, device_id_type=MESH,
         )
 
+    named_copy = pltpu.make_async_copy(named_in, named, named_sem)
+    named_copy.start()
+    parts = pn.blocks // 4
+    point_copies = [
+        pltpu.make_async_copy(
+            points_in.at[pl.ds(k * parts, parts)], points.at[pl.ds(k * parts, parts)], pts_sem.at[k]
+        )
+        for k in range(4)
+    ]
+    for copy in point_copies:
+        copy.start()
+    own_copy = pltpu.make_async_copy(cent_in.at[c], cents.at[side], cent_sem)
+    own_copy.start()
+
     barrier = pltpu.get_barrier_semaphore()
     for mask in range(1, Q):
         pl.semaphore_signal(barrier, inc=1, device_id=device(flip(q, mask)), device_id_type=MESH)
     pl.semaphore_signal(barrier, inc=1, device_id=partner, device_id_type=MESH)
-    own_copy = pltpu.make_async_copy(cent_in.at[c], cents.at[side], cent_sem)
-    own_copy.start()
+    named_copy.wait()
+
+    entries = 2 * pn.blocks
+    picked = jnp.concatenate([named[0:1], named[1:2]], axis=1).astype(jnp.float32)
+    member = picked == iota((pn.total, entries), 0).astype(jnp.float32)
+    earlier = (iota((entries, entries), 0) < iota((entries, entries), 1)).astype(jnp.bfloat16)
+    prior = jnp.dot(member.astype(jnp.bfloat16), earlier, preferred_element_type=jnp.float32)
+    turn = jnp.sum(jnp.where(member, prior, 0.0), axis=0, keepdims=True)
+    holder = iota((pn.total, entries), 1) % pn.blocks + 1
+    homes = [
+        jnp.sum(jnp.where(member & (turn == float(t)), holder, 0).astype(jnp.float32), axis=1, keepdims=True) - 1.0
+        for t in range(pn.cap)
+    ]
+    grid = jnp.zeros((pn.total, LANES), jnp.int32)
+    for t in range(pn.cap):
+        grid = jnp.where(iota(grid.shape, 1) == t, jnp.maximum(homes[t], 0.0).astype(jnp.int32), grid)
+    home_v[...] = grid
+    home_copy = pltpu.make_async_copy(home_v, home, home_sem)
 
     masks = [2 * pair + low for pair in pn.pair_order() for low in (0, 1)]
+
+    def point_block(block, t):
+        return points[jnp.clip(home[block, t], 0, pn.blocks - 1)]
 
     def gather(mask):
         spot = flip(q, mask)
         for sel in range(2):
-            first = (sel * Q + spot) * pn.cap
-
-            @pl.loop(0, pn.cap, unroll=pn.cap)
-            def _(t):
-                stage[mask, sel, t] = points[home[first + t]]
+            for t in range(pn.cap):
+                stage[mask, sel, t] = point_block(sel * Q + spot, t)
 
     def gather_own():
         for sel in range(2):
-            first = (sel * Q + q) * pn.cap
-            if pn.main:
-                @pl.loop(0, pn.main)
-                def _(t):
-                    recv[sel, q * pn.main + t] = points[home[first + t]]
-            if pn.rem:
-                @pl.loop(0, pn.rem)
-                def _(t):
-                    recv[sel, Q * pn.main + q * pn.rem + t] = points[home[first + pn.main + t]]
+            for t in range(pn.main):
+                recv[sel, q * pn.main + t] = point_block(sel * Q + q, t)
+            for t in range(pn.rem):
+                recv[sel, Q * pn.main + q * pn.rem + t] = point_block(sel * Q + q, pn.main + t)
 
     def main_copy(mask, sel, spot_at):
         return remote(
@@ -168,6 +193,10 @@
             if pn.rem:
                 rem_copy(mask, sel, q).start()
 
+    for copy in point_copies:
+        copy.wait()
+    home_copy.start()
+    home_copy.wait()
     waiting = None
     for mask in masks:
         if mask:
@@ -184,11 +213,16 @@
     cent_wait = remote(cents.at[other], cents.at[other], cs, cr, partner)
     gather_own()
 
-    lanes = table[...].astype(jnp.float32)
-    entries = 2 * pn.blocks
-    entry_row = to_column(lanes[0:1], 0, entries)
-    entry_lane = to_column(lanes[1:2], 0, entries)
-    slot_home = to_column(lanes[2:3], 0, pn.slots)
+    upper = (picked >= float(Q)).astype(jnp.float32)
+    spot_row = picked - float(Q) * upper
+    eighth = jnp.floor(turn * (1.0 / GROUP))
+    in_main = turn < float(pn.main)
+    row = spot_row * 8.0 + upper * float(pn.rows) + jnp.where(in_main, eighth, float(pn.main_rows))
+    mine = ((q % pn.share) * pn.rem - pn.main).astype(jnp.float32)
+    lane = jnp.where(in_main, turn - GROUP * eighth, turn + mine)
+    entry_row = to_column(row, 0, entries)
+    entry_lane = to_column(lane, 0, entries)
+    slot_home = jnp.concatenate(homes, axis=0)
     pick[...] = (entry_row == iota((entries, 8 * Q), 1).astype(jnp.float32)).astype(jnp.bfloat16)
     lane_group = (iota((entries, LANES), 1) // PB).astype(jnp.float32)
     pick_lane[...] = (entry_lane == lane_group).astype(jnp.float32)
@@ -436,43 +470,15 @@
             f_copy(step, k, (c - step + pn.cent) % pn.cent).wait_recv()
 
 
-def tables(pn, candidates):
-    q = (lax.axis_index("pts") % pn.half) * pn.cent + lax.axis_index("cent")
-    picked = candidates.T.reshape(-1)
-    count = picked.shape[0]
-    index = jnp.arange(count, dtype=jnp.int32)
-    labels = jnp.arange(pn.total, dtype=jnp.int32)
-    member = (picked[:, None] == labels[None, :]).astype(jnp.bfloat16)
-    earlier = (index[None, :] < index[:, None]).astype(jnp.bfloat16)
-    prior = jnp.dot(earlier, member, preferred_element_type=jnp.float32)
-    turn = jnp.sum(prior * member.astype(jnp.float32), axis=1).astype(jnp.int32)
-    place = picked * pn.cap + turn
-    spot, sel = picked % pn.spots, picked // pn.spots
-    in_main = turn < pn.main
-    row = spot * 8 + sel * pn.rows + jnp.where(in_main, turn // GROUP, pn.main_rows)
-    lane = jnp.where(in_main, turn % GROUP, (q % pn.share) * pn.rem + turn - pn.main)
-    places = jnp.arange(pn.slots, dtype=jnp.int32)
-    block = index % pn.blocks
-    source = jnp.sum(jnp.where(place[:, None] == places[None, :], block[:, None] + 1, 0), axis=0) - 1
-    by_turn = source.reshape(pn.total, pn.cap).T.reshape(-1)
-    width = -(-max(count, pn.slots) // LANES) * LANES
-
-    def row_of(values):
-        return jnp.pad(values, (0, width - values.shape[0]))[None]
-
-    rows = jnp.concatenate([row_of(row), row_of(lane), row_of(by_turn)], axis=0)
-    table = jnp.pad(rows, ((0, 5), (0, 0)))
-    return jnp.maximum(source, 0), table
-
-
 def on_device(points, centroids, candidates):
     width = points.shape[1]
     pn = Plan(lax.axis_size("pts"), lax.axis_size("cent"), candidates.shape[0], width)
     assert centroids.shape[0] == pn.cent * CB
-    home, table = tables(pn, candidates)
     Q, bf16, f32 = pn.spots, jnp.bfloat16, jnp.float32
     vmem = pl.BlockSpec(memory_space=pltpu.VMEM)
+    hbm = pl.BlockSpec(memory_space=pltpu.HBM)
     dma = pltpu.SemaphoreType.DMA
+    early = [((2, pn.blocks), jnp.int32), ((pn.blocks, PB, width), bf16), ((pn.total, LANES), jnp.int32)]
     buffers = [
         ((Q, 2, pn.cap, PB, width), bf16),
         ((2, pn.held, PB, width), bf16),
@@ -501,16 +507,20 @@
         ((8, CB), f32),
         ((8, CB), f32),
     ]
-    taken = sum(math.prod(shape) * jnp.dtype(kind).itemsize for shape, kind in buffers)
+    taken = sum(math.prod(shape) * jnp.dtype(kind).itemsize for shape, kind in early + buffers)
     new, lse = pl.pallas_call(
         functools.partial(kernel, pn, 1.0 / math.sqrt(width)),
         out_shape=(
             jax.ShapeDtypeStruct((pn.cent, CB, width), bf16),
             jax.ShapeDtypeStruct((pn.blocks // GROUP, LANES), f32),
         ),
-        in_specs=[pl.BlockSpec(memory_space=pltpu.SMEM), vmem, vmem, pl.BlockSpec(memory_space=pl.ANY)],
+        in_specs=[hbm, hbm, hbm],
         out_specs=(vmem, vmem),
-        scratch_shapes=[pltpu.VMEM(*buffer) for buffer in buffers] + [
+        scratch_shapes=[pltpu.VMEM(*buffer) for buffer in early]
+        + [pltpu.SMEM((pn.total, LANES), jnp.int32)]
+        + [pltpu.VMEM(*buffer) for buffer in buffers]
+        + [
+            dma, dma((4,)), dma,
             dma((Q, 2)), dma((Q, 2)), dma((Q, 2)), dma((Q, 2)),
             dma, dma, dma,
             dma((ITERS, Q)), dma((ITERS, Q)), dma((ITERS, Q)), dma((ITERS, Q)),
@@ -521,7 +531,11 @@
         compiler_params=pltpu.CompilerParams(
             collective_id=0, has_side_effects=True, vmem_limit_bytes=taken + SPARE
         ),
-    )(home, table, points.reshape(pn.blocks, PB, width), centroids.reshape(pn.cent, CB, width))
+    )(
+        pltpu.with_memory_space_constraint(candidates.T, pltpu.HBM),
+        pltpu.with_memory_space_constraint(points.reshape(pn.blocks, PB, width), pltpu.HBM),
+        pltpu.with_memory_space_constraint(centroids.reshape(pn.cent, CB, width), pltpu.HBM),
+    )
     return new.reshape(centroids.shape), lse.reshape(-1)
 
 

time: 147 us -> 142 us (0.966)
  local copies, waits for them, and re-layouts: 4.67 us -> 1.57 us
    unnamed x6 -> x2, local copies, waits for them, and re-layouts: 4.38 us -> 1.57 us
where the time goes in v3:
time: 142 us
  Pallas kernels  139 us (98%)
  local copies, waits for them, and re-layouts  1.57 us (1%)
    pallas_call x1, Pallas kernels, on_device(): pl.pallas_call(functools.partial(kernel, pn, 1.0 / math.sqrt(width)), out...  139 us

profile of v3, /device:TPU:0, one launch (start us, length us, event | category | flops | bytes accessed | tf_op | source)
XLA Modules:
  0.0 141.6 jit_solution(10311170917034516460)
XLA Ops:
  0.6 139.4 %shard_map.50 = (bf16[4,256,512]{2,1,0:T(8,128)(2,1)S(1)}, f32[16,128]{1,0:T(8,128)S(1)}) custom-call(s32[2,128]{1,0:T(2,128)} %bitcast.9, bf16[128,16,512]{2,1,0:T(8,128)(2,1)} %bitcast.7, bf16[4,256,512]{2,1,0:T(8,128)(2,1)} %bitcast.8), custom_call_target="tpu_custom_call" | custom-call | tf_op jit(solution)/shard_map/pallas_call | solution.py:511
  140.0 1.0 copy.7
  141.0 0.6 copy.8

commit v4 on v3

--- a/solution.py
+++ b/solution.py
@@ -39,7 +39,7 @@
         self.tiles = self.groups // 2
         self.tile_blocks = 2 * GROUP
         assert GROUP % max(self.rem, 1) == 0 and 2 * self.rows <= 8
-        assert self.spots & (self.spots - 1) == 0 and self.held % self.tile_blocks == 0
+        assert self.cent % 2 == 0 and self.spots & (self.spots - 1) == 0 and self.held % self.tile_blocks == 0
 
     def pair_order(self):
         pairs = self.spots // 2
@@ -269,11 +269,6 @@
             for s in range(pn.share):
                 row = (first + s) * 8 + sel * pn.rows + pn.main_rows
                 pmsg[it, pl.ds(row, 1)] = part
-
-    def score_all_rem(it, sel):
-        @pl.loop(main_tiles, pn.tiles)
-        def _(tile):
-            score_rem(it, sel, tile)
 
     def trade(out, into, send_sem, recv_sem, it):
         into[it, pl.ds(q * 8, 8)] = out[it, pl.ds(q * 8, 8)]
@@ -355,33 +350,19 @@
     cent_wait.wait_recv()
     set_norm(other)
 
-    def wait_main(mask):
-        spot = flip(q, mask)
-        for sel in range(2):
-            main_copy(mask, sel, spot).wait_recv()
-
-    for pair in pn.pair_order()[-1:] + pn.pair_order()[:-1]:
-        if pn.main:
-            for low in (0, 1):
-                if 2 * pair + low:
-                    wait_main(2 * pair + low)
-            if pn.main_rows == 1:
-                tile = flip(q, 2 * pair) // 2
-
-                for sel in range(2):
-                    score_main(0, sel, tile)
-    if pn.main_rows > 1:
-        for sel in range(2):
-            @pl.loop(0, main_tiles)
-            def _(tile):
-                score_main(0, sel, tile)
-    if pn.rem:
-        for mask in masks:
-            if mask:
-                for sel in range(2):
+    def score_all(it, sel):
+        for tile in range(pn.tiles):
+            (score_main if tile < main_tiles else score_rem)(it, sel, tile)
+
+    for mask in masks:
+        if mask:
+            for sel in range(2):
+                if pn.main:
+                    main_copy(mask, sel, flip(q, mask)).wait_recv()
+                if pn.rem:
                     rem_copy(mask, sel, flip(q, mask)).wait_recv()
-        for sel in range(2):
-            score_all_rem(0, sel)
+    for sel in range(2):
+        score_all(0, sel)
     trade(pmsg, pin, ps, pr, 0)
     combine(0)
     trade(lmsg, lin, ls, lr, 0)
@@ -411,12 +392,7 @@
         both = xout[sel].astype(jnp.float32) + xin[sel].astype(jnp.float32)
         cents[sel] = renewed(both, mass, cents[sel])
         set_norm(sel)
-        if pn.main:
-            @pl.loop(0, main_tiles, unroll=2)
-            def _(tile):
-                score_main(1, sel, tile)
-        if pn.rem:
-            score_all_rem(1, sel)
+        score_all(1, sel)
 
     trade(pmsg, pin, ps, pr, 1)
     combine(1)
@@ -439,18 +415,28 @@
     m2_copy.wait_recv()
     mass = mass + to_column(min2[0:1], 0, CB)
 
-    def f_copy(step, k, spot):
+    pairs = pn.cent // 2
+    beside = c + 1 - 2 * (c % 2)
+
+    def away(step):
+        return (c + 2 * step) % pn.cent
+
+    def f_copy(number, k, spot, to):
         part = new_out.at[spot, pl.ds(k * rows, rows)]
-        to = {"pts": p, "cent": (c + step) % pn.cent}
-        return remote(part, part, fs.at[step, k], fr.at[spot, k], to)
+        return remote(part, part, fs.at[number, k], fr.at[spot, k], {"pts": p, "cent": to})
 
     for k in range(CHUNKS):
         part = pl.ds(k * rows, rows)
         x2_copy(k).wait_recv()
         sums = acc[part] + xin2[part].astype(jnp.float32)
         new_out[c, part] = renewed(sums, mass[k * rows : (k + 1) * rows], cents[side, part])
-        for step in range(1, pn.cent):
-            f_copy(step, k, c).start()
+        for step in range(1, pairs):
+            f_copy(step, k, c, away(step)).start()
+        f_copy(0, k, c, beside).start()
+    for k in range(CHUNKS):
+        for step in range(1, pairs):
+            f_copy(step, k, away(pairs - step), c).wait_recv()
+            f_copy(pairs + step - 1, k, away(pairs - step), beside).start()
 
     for mask in masks:
         if mask:
@@ -465,9 +451,12 @@
     m2_copy.wait_send()
     for k in range(CHUNKS):
         x2_copy(k).wait_send()
-        for step in range(1, pn.cent):
-            f_copy(step, k, c).wait_send()
-            f_copy(step, k, (c - step + pn.cent) % pn.cent).wait_recv()
+        f_copy(0, k, c, beside).wait_send()
+        f_copy(0, k, beside, c).wait_recv()
+        for step in range(1, pairs):
+            f_copy(step, k, c, away(step)).wait_send()
+            f_copy(pairs + step - 1, k, away(pairs - step), beside).wait_send()
+            f_copy(0, k, (beside + 2 * (pairs - step)) % pn.cent, c).wait_recv()
 
 
 def on_device(points, centroids, candidates):

time: 142 us -> 134 us (0.944)
  Pallas kernels: 139 us -> 132 us
    pallas_call x1, Pallas kernels: 139 us -> 132 us  [on_device(): pl.pallas_call(functools.partial(kernel, pn, 1.0 / math.sqrt(width)), out...]
where the time goes in v4:
time: 134 us
  Pallas kernels  132 us (99%)
  local copies, waits for them, and re-layouts  1.57 us (1%)
    pallas_call x1, Pallas kernels, on_device(): pl.pallas_call(functools.partial(kernel, pn, 1.0 / math.sqrt(width)), out...  132 us

profile of v4, /device:TPU:0, one launch (start us, length us, event | category | flops | bytes accessed | tf_op | source)
XLA Modules:
  0.0 134.1 jit_solution(6610716631886055258)
XLA Ops:
  0.6 131.9 %shard_map.50 = (bf16[4,256,512]{2,1,0:T(8,128)(2,1)S(1)}, f32[16,128]{1,0:T(8,128)S(1)}) custom-call(s32[2,128]{1,0:T(2,128)} %bitcast.9, bf16[128,16,512]{2,1,0:T(8,128)(2,1)} %bitcast.7, bf16[4,256,512]{2,1,0:T(8,128)(2,1)} %bitcast.8), custom_call_target="tpu_custom_call" | custom-call | tf_op jit(solution)/shard_map/pallas_call | solution.py:500
  132.5 1.0 copy.7
  133.5 0.6 copy.8

commit v5 on v4

--- a/solution.py
+++ b/solution.py
@@ -193,6 +193,10 @@
             if pn.rem:
                 rem_copy(mask, sel, q).start()
 
+    own_copy.wait()
+    pl.semaphore_wait(barrier, Q)
+    cent_copy = remote(cents.at[side], cents.at[side], cs, cr, partner)
+    cent_copy.start()
     for copy in point_copies:
         copy.wait()
     home_copy.start()
@@ -201,15 +205,10 @@
     for mask in masks:
         if mask:
             gather(mask)
-            if waiting is None:
-                pl.semaphore_wait(barrier, Q)
-            else:
+            if waiting is not None:
                 send(waiting)
             waiting = mask
-    own_copy.wait()
     send(waiting)
-    cent_copy = remote(cents.at[side], cents.at[side], cs, cr, partner)
-    cent_copy.start()
     cent_wait = remote(cents.at[other], cents.at[other], cs, cr, partner)
     gather_own()
 

time: 134 us -> 133 us (level)
  Pallas kernels: 132 us -> 130 us
    pallas_call x1, Pallas kernels: 132 us -> 130 us  [on_device(): pl.pallas_call(functools.partial(kernel, pn, 1.0 / math.sqrt(width)), out...]
where the time goes in v5:
time: 133 us; the launch traced here: 132 us
  Pallas kernels  130 us (98%)
  local copies, waits for them, and re-layouts  1.57 us (1%)
    pallas_call x1, Pallas kernels, on_device(): pl.pallas_call(functools.partial(kernel, pn, 1.0 / math.sqrt(width)), out...  130 us

profile of v5, /device:TPU:0, one launch (start us, length us, event | category | flops | bytes accessed | tf_op | source)
XLA Modules:
  0.0 132.5 jit_solution(7150735605092876977)
XLA Ops:
  0.6 130.3 %shard_map.50 = (bf16[4,256,512]{2,1,0:T(8,128)(2,1)S(1)}, f32[16,128]{1,0:T(8,128)S(1)}) custom-call(s32[2,128]{1,0:T(2,128)} %bitcast.9, bf16[128,16,512]{2,1,0:T(8,128)(2,1)} %bitcast.7, bf16[4,256,512]{2,1,0:T(8,128)(2,1)} %bitcast.8), custom_call_target="tpu_custom_call" | custom-call | tf_op jit(solution)/shard_map/pallas_call | solution.py:499
  130.9 1.0 copy.7
  131.9 0.6 copy.8
